TPU v7x, 32 devices: a whole 2x2x4 slice. The times are simulated.
32 devices in a mesh: dp: 8 (over z, y), tensor: 4 (over x, core).
Axes of the slice: x: 2, y: 2, z: 4, core: 2. Of those that a mesh axis runs over, the one named last changes fastest.
Arguments:
- tokens: bfloat16 [8192, 2048], P(('dp', 'tensor')), may hold values from -6 to 6
- norm_gain: bfloat16 [2048], replicated, may hold values from 0.5 to 1.5
- norm_bias: bfloat16 [2048], replicated, may hold values from -3 to 3
- query_weight: bfloat16 [2048, 2048], P('dp', 'tensor'), may hold values from -0.1875 to 0.1875
- query_bias: bfloat16 [2048], P('tensor'), may hold values from -3 to 3
- key_weight: bfloat16 [2048, 2048], P('dp', 'tensor'), may hold values from -0.1875 to 0.1875
- key_bias: bfloat16 [2048], P('tensor'), may hold values from -3 to 3
- value_weight: bfloat16 [2048, 2048], P('dp', 'tensor'), may hold values from -0.125 to 0.125
- value_bias: bfloat16 [2048], P('tensor'), may hold values from -3 to 3
- output_weight: bfloat16 [2048, 2048], P('tensor', 'dp'), may hold values from -0.5 to 0.5
- output_bias: bfloat16 [2048], replicated, may hold values from -3 to 3
- up_weight: bfloat16 [2048, 8192], P('dp', 'tensor'), may hold values from -0.125 to 0.125
- up_bias: bfloat16 [8192], P('tensor'), may hold values from -3 to 3
- down_weight: bfloat16 [8192, 2048], P('tensor', 'dp'), may hold values from -0.0625 to 0.0625
- down_bias: bfloat16 [2048], replicated, may hold values from -3 to 3
- doc_split: int32 [8], P('dp'), may hold values from 256 to 768, as said below
- cotangent: bfloat16 [8192, 2048], P(('dp', 'tensor')), may hold values from -6 to 6
Outputs:
- out: bfloat16 [8192, 2048], P(('dp', 'tensor'))
- grad_tokens: float32 [8192, 2048], P(('dp', 'tensor'))
- grad_norm_gain: float32 [2048], replicated
- grad_norm_bias: float32 [2048], replicated
- grad_query_weight: float32 [2048, 2048], P('dp', 'tensor')
- grad_query_bias: float32 [2048], P('tensor')
- grad_key_weight: float32 [2048, 2048], P('dp', 'tensor')
- grad_key_bias: float32 [2048], P('tensor')
- grad_value_weight: float32 [2048, 2048], P('dp', 'tensor')
- grad_value_bias: float32 [2048], P('tensor')
- grad_output_weight: float32 [2048, 2048], P('tensor', 'dp')
- grad_output_bias: float32 [2048], replicated
- grad_up_weight: float32 [2048, 8192], P('dp', 'tensor')
- grad_up_bias: float32 [8192], P('tensor')
- grad_down_weight: float32 [8192, 2048], P('tensor', 'dp')
- grad_down_bias: float32 [2048], replicated
Inputs may be any that keep to these rules, and one draw needn't show every extreme that they name: `doc_split`: each sequence holds two documents; the second begins at a multiple of 256, and every such start from 256 to 768 occurs in some sequence.
All inputs are finite; a program needn't handle non-finite values.
Results may differ from a plain program's by a relative error of at most 0.013.
The roundings to bfloat16 on the way count: a program that leaves them out, or rounds other values in their place, can miss the bound.
Values may be sent and summed in bfloat16 or wider, within the bound.
A program may use at most 256 MiB of HBM per device.

v0:
```python
import jax
import jax.numpy as jnp
from jax import lax
from jax.sharding import PartitionSpec as P

HEADS = 32
HEAD_DIM = 64
ROT = 32
BLOCK = 256
SEQ = 1024
EPS = 1e-05
NEG = -1000000000.0


def tables(split_at, seq_len):
    token_index = jnp.arange(seq_len, dtype=jnp.int32)
    later_doc = token_index >= split_at
    position = (token_index - jnp.where(later_doc, split_at, 0)).astype(jnp.float32)
    frequency = 10000.0 ** (-(2.0 * jnp.arange(ROT // 2, dtype=jnp.float32)) / ROT)
    angles = position[:, None] * frequency[None, :]
    return (jnp.cos(angles), jnp.sin(angles), later_doc)


def rotate(values, cosine, sine_table):
    half_rot = ROT // 2
    front_part = values[..., :half_rot]
    back_part = values[..., half_rot:ROT]
    cos_wide = cosine[..., None, :]
    sin_wide = sine_table[..., None, :]
    return jnp.concatenate(
        [
            front_part * cos_wide - back_part * sin_wide,
            back_part * cos_wide + front_part * sin_wide,
            values[..., ROT:],
        ],
        axis=-1,
    )


def rotate_back(grads, cosine, sine_table):
    half_rot = ROT // 2
    front_part = grads[..., :half_rot]
    back_part = grads[..., half_rot:ROT]
    cos_wide = cosine[..., None, :]
    sin_wide = sine_table[..., None, :]
    return jnp.concatenate(
        [
            front_part * cos_wide + back_part * sin_wide,
            back_part * cos_wide - front_part * sin_wide,
            grads[..., ROT:],
        ],
        axis=-1,
    )


def contract_last(left, right):
    return lax.dot_general(
        left, right, (((1,), (1,)), ((), ())), preferred_element_type=jnp.float32
    )


def contract_first(left, right):
    return lax.dot_general(
        left, right, (((0,), (0,)), ((), ())), preferred_element_type=jnp.float32
    )


def block_layout(split_at, seq_len):
    token_index = jnp.arange(seq_len, dtype=jnp.int32)
    return (token_index // BLOCK, token_index >= split_at)


def attend(queries, keys_rot, values_all, split_at):
    seq_len, heads_here, head_size = queries.shape
    rows_step = min(512, seq_len)
    step_count = seq_len // rows_step
    block_ids, later_doc = block_layout(split_at, seq_len)
    scale = HEAD_DIM ** (-0.5)

    def one_block(block_item):
        query_rows, row_blocks, row_docs = block_item
        allowed = (block_ids[None, :] <= row_blocks[:, None]) & (
            later_doc[None, :] == row_docs[:, None]
        )
        raw_scores = jnp.einsum(
            "qhd,khd->hqk", query_rows, keys_rot, preferred_element_type=jnp.float32
        )
        scores = jnp.where(allowed[None], raw_scores * scale, NEG)
        row_top = jnp.max(scores, -1, keepdims=True)
        exponent = jnp.exp(scores - row_top)
        row_total = jnp.sum(exponent, -1, keepdims=True)
        probability = (exponent / row_total).astype(jnp.bfloat16)
        attended = jnp.einsum(
            "hqk,khd->qhd", probability, values_all, preferred_element_type=jnp.float32
        )
        return (attended.astype(jnp.bfloat16), (row_top + jnp.log(row_total))[..., 0])

    attended, log_totals = lax.map(
        one_block,
        (
            queries.reshape(step_count, rows_step, heads_here, head_size),
            block_ids.reshape(step_count, rows_step),
            later_doc.reshape(step_count, rows_step),
        ),
    )
    return (attended.reshape(seq_len, heads_here, head_size), log_totals)


def attend_back(queries, keys_rot, values_all, grad_attended, log_totals, split_at):
    seq_len, heads_here, head_size = queries.shape
    rows_step = min(512, seq_len)
    step_count = seq_len // rows_step
    block_ids, later_doc = block_layout(split_at, seq_len)
    scale = HEAD_DIM ** (-0.5)

    def one_block(running, block_item):
        key_acc, value_acc = running
        query_rows, grad_rows, log_rows, row_blocks, row_docs = block_item
        allowed = (block_ids[None, :] <= row_blocks[:, None]) & (
            later_doc[None, :] == row_docs[:, None]
        )
        raw_scores = jnp.einsum(
            "qhd,khd->hqk", query_rows, keys_rot, preferred_element_type=jnp.float32
        )
        scores = jnp.where(allowed[None], raw_scores * scale, NEG)
        probability = jnp.exp(scores - log_rows[..., None])
        grad_prob = jnp.einsum(
            "qhd,khd->hqk", grad_rows, values_all, preferred_element_type=jnp.float32
        )
        row_dot = jnp.sum(probability * grad_prob, -1, keepdims=True)
        grad_scores = (probability * (grad_prob - row_dot) * scale).astype(jnp.bfloat16)
        grad_query = jnp.einsum(
            "hqk,khd->qhd", grad_scores, keys_rot, preferred_element_type=jnp.float32
        )
        key_acc = key_acc + jnp.einsum(
            "hqk,qhd->khd", grad_scores, query_rows, preferred_element_type=jnp.float32
        )
        value_acc = value_acc + jnp.einsum(
            "hqk,qhd->khd",
            probability.astype(jnp.bfloat16),
            grad_rows,
            preferred_element_type=jnp.float32,
        )
        return ((key_acc, value_acc), grad_query)

    zeros_kv = jnp.zeros((seq_len, heads_here, head_size), jnp.float32)
    (grad_keys, grad_values), grad_queries = lax.scan(
        one_block,
        (zeros_kv, zeros_kv),
        (
            queries.reshape(step_count, rows_step, heads_here, head_size),
            grad_attended.reshape(step_count, rows_step, heads_here, head_size),
            log_totals,
            block_ids.reshape(step_count, rows_step),
            later_doc.reshape(step_count, rows_step),
        ),
    )
    return (grad_queries.reshape(seq_len, heads_here, head_size), grad_keys, grad_values)


def gelu_tanh(hidden):
    return jax.nn.gelu(hidden, approximate=True)


def on_device(
    tokens,
    norm_gain,
    norm_bias,
    query_weight,
    query_bias,
    key_weight,
    key_bias,
    value_weight,
    value_bias,
    output_weight,
    output_bias,
    up_weight,
    up_bias,
    down_weight,
    down_bias,
    doc_split,
    cotangent,
):
    heads_here = HEADS // lax.axis_size("tensor")
    width_here = heads_here * HEAD_DIM
    seq_count = doc_split.shape[0]
    gain_wide = norm_gain.astype(jnp.float32)
    tokens_wide = tokens.astype(jnp.float32)
    row_mean = jnp.mean(tokens_wide, -1, keepdims=True)
    centred = tokens_wide - row_mean
    inv_scale = lax.rsqrt(jnp.mean(centred * centred, -1, keepdims=True) + EPS)
    standard = centred * inv_scale
    normed = (standard * gain_wide + norm_bias.astype(jnp.float32)).astype(jnp.bfloat16)
    normed_all = lax.all_gather(normed, "tensor", axis=0, tiled=True)
    full_query, full_key, full_value, full_up = (
        lax.all_gather(query_weight, "dp", axis=0, tiled=True),
        lax.all_gather(key_weight, "dp", axis=0, tiled=True),
        lax.all_gather(value_weight, "dp", axis=0, tiled=True),
        lax.all_gather(up_weight, "dp", axis=0, tiled=True),
    )
    full_output, full_down = (
        lax.all_gather(output_weight, "dp", axis=1, tiled=True),
        lax.all_gather(down_weight, "dp", axis=1, tiled=True),
    )
    rows_all = normed_all.shape[0]
    q_pre = jnp.dot(normed_all, full_query, preferred_element_type=jnp.float32) + query_bias.astype(
        jnp.float32
    )
    k_pre = jnp.dot(normed_all, full_key, preferred_element_type=jnp.float32) + key_bias.astype(
        jnp.float32
    )
    v_pre = jnp.dot(normed_all, full_value, preferred_element_type=jnp.float32) + value_bias.astype(
        jnp.float32
    )
    hidden = jnp.dot(normed_all, full_up, preferred_element_type=jnp.float32) + up_bias.astype(
        jnp.float32
    )
    cosine, sine_table, later_unused = jax.vmap(lambda split_at: tables(split_at, SEQ))(doc_split)
    shaped = (seq_count, SEQ, heads_here, HEAD_DIM)
    queries = rotate(q_pre.reshape(shaped), cosine, sine_table).astype(jnp.bfloat16)
    keys_rot = rotate(k_pre.reshape(shaped), cosine, sine_table).astype(jnp.bfloat16)
    values_all = v_pre.astype(jnp.bfloat16).reshape(shaped)
    attended, log_totals = lax.map(
        lambda seq_item: attend(*seq_item), (queries, keys_rot, values_all, doc_split)
    )
    attended_flat = attended.reshape(rows_all, width_here)
    activated = gelu_tanh(hidden).astype(jnp.bfloat16)
    partial_out = jnp.dot(attended_flat, full_output, preferred_element_type=jnp.float32) + jnp.dot(
        activated, full_down, preferred_element_type=jnp.float32
    )
    mixed = lax.psum_scatter(
        partial_out.astype(jnp.bfloat16), "tensor", scatter_dimension=0, tiled=True
    ).astype(jnp.float32)
    out_bias = output_bias.astype(jnp.float32) + down_bias.astype(jnp.float32)
    out = (tokens_wide + mixed + out_bias).astype(jnp.bfloat16)
    cot_all = lax.all_gather(cotangent, "tensor", axis=0, tiled=True)
    grad_attn_wide = contract_last(cot_all, full_output)
    grad_activated = contract_last(cot_all, full_down)
    grad_attn = grad_attn_wide.astype(jnp.bfloat16)
    grad_hidden = jax.vjp(gelu_tanh, hidden)[1](grad_activated)[0].astype(jnp.bfloat16)
    grad_queries, grad_keys, grad_values = lax.map(
        lambda seq_item: attend_back(*seq_item),
        (queries, keys_rot, values_all, grad_attn.reshape(shaped), log_totals, doc_split),
    )
    grad_q = (
        rotate_back(grad_queries, cosine, sine_table)
        .reshape(rows_all, width_here)
        .astype(jnp.bfloat16)
    )
    grad_k = (
        rotate_back(grad_keys, cosine, sine_table)
        .reshape(rows_all, width_here)
        .astype(jnp.bfloat16)
    )
    grad_v = grad_values.reshape(rows_all, width_here).astype(jnp.bfloat16)
    grad_normed_part = (
        contract_last(grad_q, full_query)
        + contract_last(grad_k, full_key)
        + contract_last(grad_v, full_value)
        + contract_last(grad_hidden, full_up)
    )
    grad_normed = lax.psum_scatter(
        grad_normed_part.astype(jnp.bfloat16), "tensor", scatter_dimension=0, tiled=True
    ).astype(jnp.float32)
    grad_query_weight, grad_key_weight, grad_value_weight, grad_up_weight = (
        lax.psum_scatter(
            contract_first(normed_all, grad_q).astype(jnp.bfloat16),
            "dp",
            scatter_dimension=0,
            tiled=True,
        ).astype(jnp.float32),
        lax.psum_scatter(
            contract_first(normed_all, grad_k).astype(jnp.bfloat16),
            "dp",
            scatter_dimension=0,
            tiled=True,
        ).astype(jnp.float32),
        lax.psum_scatter(
            contract_first(normed_all, grad_v).astype(jnp.bfloat16),
            "dp",
            scatter_dimension=0,
            tiled=True,
        ).astype(jnp.float32),
        lax.psum_scatter(
            contract_first(normed_all, grad_hidden).astype(jnp.bfloat16),
            "dp",
            scatter_dimension=0,
            tiled=True,
        ).astype(jnp.float32),
    )
    grad_output_weight, grad_down_weight = (
        lax.psum_scatter(
            contract_first(attended_flat, cot_all).astype(jnp.bfloat16),
            "dp",
            scatter_dimension=1,
            tiled=True,
        ).astype(jnp.float32),
        lax.psum_scatter(
            contract_first(activated, cot_all).astype(jnp.bfloat16),
            "dp",
            scatter_dimension=1,
            tiled=True,
        ).astype(jnp.float32),
    )
    grad_query_bias, grad_key_bias, grad_value_bias, grad_up_bias = lax.psum(
        (
            jnp.sum(grad_q, 0, dtype=jnp.float32),
            jnp.sum(grad_k, 0, dtype=jnp.float32),
            jnp.sum(grad_v, 0, dtype=jnp.float32),
            jnp.sum(grad_hidden, 0, dtype=jnp.float32),
        ),
        "dp",
    )
    cot_wide = cotangent.astype(jnp.float32)
    grad_scaled = grad_normed * gain_wide
    grad_tokens = cot_wide + inv_scale * (
        grad_scaled
        - jnp.mean(grad_scaled, -1, keepdims=True)
        - standard * jnp.mean(grad_scaled * standard, -1, keepdims=True)
    )
    grad_norm_gain, grad_norm_bias, grad_out_bias = lax.psum(
        (jnp.sum(grad_normed * standard, 0), jnp.sum(grad_normed, 0), jnp.sum(cot_wide, 0)),
        ("dp", "tensor"),
    )
    return (
        out,
        grad_tokens,
        grad_norm_gain,
        grad_norm_bias,
        grad_query_weight,
        grad_query_bias,
        grad_key_weight,
        grad_key_bias,
        grad_value_weight,
        grad_value_bias,
        grad_output_weight,
        grad_out_bias,
        grad_up_weight,
        grad_up_bias,
        grad_down_weight,
        grad_out_bias,
    )


def solution(mesh):
    in_specs = (
        P(("dp", "tensor"), None),
        P(),
        P(),
        P("dp", "tensor"),
        P("tensor"),
        P("dp", "tensor"),
        P("tensor"),
        P("dp", "tensor"),
        P("tensor"),
        P("tensor", "dp"),
        P(),
        P("dp", "tensor"),
        P("tensor"),
        P("tensor", "dp"),
        P(),
        P("dp"),
        P(("dp", "tensor"), None),
    )
    out_specs = (
        P(("dp", "tensor"), None),
        P(("dp", "tensor"), None),
        P(),
        P(),
        P("dp", "tensor"),
        P("tensor"),
        P("dp", "tensor"),
        P("tensor"),
        P("dp", "tensor"),
        P("tensor"),
        P("tensor", "dp"),
        P(),
        P("dp", "tensor"),
        P("tensor"),
        P("tensor", "dp"),
        P(),
    )
    return jax.shard_map(
        on_device, mesh=mesh, in_specs=in_specs, out_specs=out_specs, check_vma=False
    )
```

profile of v0, /device:TPU:0, one launch (start us, length us, event | category | flops | bytes accessed | tf_op | source)
XLA Modules:
  0.0 1225.4 jit_solution(8028844312723084863)
XLA Ops:
  13.1 2.7 fusion.79
  20.9 41.0 %all-gather.11.cloned.1.call-done = bf16[2048,512]{1,0:T(8,128)(2,1)} async-done(((bf16[256,512]{1,0:T(8,128)(2,1)}), bf16[2048,512]{1,0:T(8,128)(2,1)}) %all-gather.11.cloned.1.call-update) | async-done | bytes 2097168 | tf_op jit(solution)/shard_map/all_gather | solution.py:196
  62.0 35.1 %all-gather.9.cloned.1.call-done = bf16[1024,2048]{1,0:T(8,128)(2,1)} async-done(((bf16[256,2048]{1,0:T(8,128)(2,1)}), bf16[1024,2048]{1,0:T(8,128)(2,1)}) %all-gather.9.cloned.1.call-update) | async-done | bytes 4194320 | tf_op jit(solution)/shard_map/all_gather | solution.py:194
  97.1 5.2 convolution_add_fusion.1
  102.4 45.9 %all-gather.13.cloned.1.call-done = bf16[2048,512]{1,0:T(8,128)(2,1)} async-done(((bf16[256,512]{1,0:T(8,128)(2,1)}), bf16[2048,512]{1,0:T(8,128)(2,1)}) %all-gather.13.cloned.1.call-update) | async-done | bytes 2097168 | tf_op jit(solution)/shard_map/all_gather | solution.py:197
  148.4 5.2 convolution_add_fusion
  158.0 41.2 %all-gather.17.cloned.1.call-done = bf16[512,2048]{1,0:T(8,128)(2,1)} async-done(((bf16[512,256]{1,0:T(8,128)(2,1)}), bf16[512,2048]{1,0:T(8,128)(2,1)}) %all-gather.17.cloned.1.call-update) | async-done | bytes 2097168 | tf_op jit(solution)/shard_map/all_gather | solution.py:202
  199.2 34.1 %all-gather.23.cloned.1.call-done = bf16[1024,2048]{1,0:T(8,128)(2,1)} async-done(((bf16[256,2048]{1,0:T(8,128)(2,1)}), bf16[1024,2048]{1,0:T(8,128)(2,1)}) %all-gather.23.cloned.1.call-update) | async-done | bytes 4194320 | tf_op jit(solution)/shard_map/all_gather | solution.py:236
  233.2 6.2 convolution_convert_fusion.6
  239.5 2.9 reshape.466
  242.4 2.2 copy.42
  246.3 2.1 pad_maximum_fusion
  248.4 36.0 %all-gather.15.cloned.1.call-done = bf16[2048,512]{1,0:T(8,128)(2,1)} async-done(((bf16[256,512]{1,0:T(8,128)(2,1)}), bf16[2048,512]{1,0:T(8,128)(2,1)}) %all-gather.15.cloned.1.call-update) | async-done | bytes 2097168 | tf_op jit(solution)/shard_map/all_gather | solution.py:198
  284.4 5.2 add_convert_fusion.2
  289.7 31.5 %while.48 = (s32[]{:T(128)}, bf16[2,512,8,64]{1,3,2,0:T(8,128)(2,1)S(1)}, f32[2,8,512]{2,1,0:T(8,128)S(1)}, s32[2,512]{1,0:T(2,128)S(1)}, pred[2,512]{1,0:T(4,12...) while((s32[]{:T(128)}, ...), condition=%wide.region_5.6_spmd.clone, body=%wide.region_2.5_spmd.clone.sunk | while | flops 1125913600 | bytes 55724152 | solution.py:98
  290.9 4.9 fusion.155
  295.8 4.2 fusion.156
  300.1 5.4 fusion.157
  306.7 4.9 fusion.155
  311.5 4.2 fusion.156
  315.8 5.4 fusion.157
  322.1 191.8 %while.49 = (s32[]{:T(128)}, f32[1024,8,64]{0,2,1:T(8,128)}, f32[1024,8,64]{0,2,1:T(8,128)}, f32[2,512,8,64]{1,0,3,2:T(2,128)}, bf16[2,512,8,64]{1,3,2,0:T(8,128...) while((s32[]{:T(128)}, f32[1024,8,64]{0,2,1:T(8,128)}, ...), condition=%wide.region_9.10_spmd.clone, body=%wide.region_7.9_spmd.clone.sunk | while | flops 2746764288 | bytes 187764448 | solution.py:147
  323.6 9.4 subtract_exponential_fusion.3
  333.0 9.5 fusion.168
  342.5 22.1 %fusion.169 = f32[1,512,8,64]{1,3,2,0:T(8,128)S(1)} fusion(bf16[1024,8,64]{0,2,1:T(8,128)(2,1)} %get-tuple-element.563, f32[8,512,1024]{2,1,0:T(8,128)} %subtract_exponential_fusion.3, f32[8,512,1024]{2,1,0:T(8,128)} %fusion.168), kind=kOutput, calls=%fused_computation.45.clone.1 | convolution fusion | flops 557847552 | bytes 35651584 | tf_op jit(solution)/shard_map/while/body/eval_jaxpr/while/body/eval_jaxpr/hqk,khd->qhd/dot_general | solution.py:132
  365.7 19.6 %dynamic_update_slice.35 = f32[2,512,8,64]{1,0,3,2:T(2,128)} dynamic-update-slice(f32[2,512,8,64]{1,0,3,2:T(2,128)} %get-tuple-element.545, f32[1,512,8,64]{1,0,3,2:T(1,128)S(1)} %copy.64, s32[]{:T(128)} %get-tuple-element.542, s32[]{:T(128)} %constant.124.clone.1..sunk, s32[]{:T(128)} %constant.124.clone.1..sunk, s32[]{:T(128)} %constant.124.clone.1..sunk) | dynamic-update-slice | bytes 2097156 | tf_op jit(solution)/shard_map/while/body/eval_jaxpr/while/body/jit(dynamic_update_index_in_dim)/dynamic_update_slice | solution.py:147
  385.3 23.5 %bitcast_add_fusion.4 = f32[1024,8,64]{0,2,1:T(8,128)} fusion(f32[1024,8,64]{0,2,1:T(8,128)} %get-tuple-element.543, f32[8,512,1024]{2,1,0:T(8,128)} %subtract_exponential_fusion.3, f32[8,512,1024]{2,1,0:T(8,128)} %fusion.168, pred[]{:T(512)S(6)} %compare.7, bf16[2,512,8,64]{1,3,2,0:T(8,128)(2,1)} %get-tuple-element.560, s32[]{:T(128)} %get-tuple-element.542), kind=kOutput, calls=%fused_computation.43.clone.1 | convolution fusion | flops 558896128 | bytes 71827968 | tf_op jit(solution)/shard_map/while/body/eval_jaxpr/while/body/eval_jaxpr/hqk,qhd->khd/dot_general | solution.py:135
  408.8 7.8 bitcast_add_fusion.5
  419.1 9.5 subtract_exponential_fusion.3
  428.6 9.1 fusion.168
  437.8 22.1 %fusion.169 = f32[1,512,8,64]{1,3,2,0:T(8,128)S(1)} fusion(bf16[1024,8,64]{0,2,1:T(8,128)(2,1)} %get-tuple-element.563, f32[8,512,1024]{2,1,0:T(8,128)} %subtract_exponential_fusion.3, f32[8,512,1024]{2,1,0:T(8,128)} %fusion.168), kind=kOutput, calls=%fused_computation.45.clone.1 | convolution fusion | flops 557847552 | bytes 35651584 | tf_op jit(solution)/shard_map/while/body/eval_jaxpr/while/body/eval_jaxpr/hqk,khd->qhd/dot_general | solution.py:132
  460.9 19.6 %dynamic_update_slice.35 = f32[2,512,8,64]{1,0,3,2:T(2,128)} dynamic-update-slice(f32[2,512,8,64]{1,0,3,2:T(2,128)} %get-tuple-element.545, f32[1,512,8,64]{1,0,3,2:T(1,128)S(1)} %copy.64, s32[]{:T(128)} %get-tuple-element.542, s32[]{:T(128)} %constant.124.clone.1..sunk, s32[]{:T(128)} %constant.124.clone.1..sunk, s32[]{:T(128)} %constant.124.clone.1..sunk) | dynamic-update-slice | bytes 2097156 | tf_op jit(solution)/shard_map/while/body/eval_jaxpr/while/body/jit(dynamic_update_index_in_dim)/dynamic_update_slice | solution.py:147
  480.6 24.3 %bitcast_add_fusion.4 = f32[1024,8,64]{0,2,1:T(8,128)} fusion(f32[1024,8,64]{0,2,1:T(8,128)} %get-tuple-element.543, f32[8,512,1024]{2,1,0:T(8,128)} %subtract_exponential_fusion.3, f32[8,512,1024]{2,1,0:T(8,128)} %fusion.168, pred[]{:T(512)S(6)} %compare.7, bf16[2,512,8,64]{1,3,2,0:T(8,128)(2,1)} %get-tuple-element.560, s32[]{:T(128)} %get-tuple-element.542), kind=kOutput, calls=%fused_computation.43.clone.1 | convolution fusion | flops 558896128 | bytes 71827968 | tf_op jit(solution)/shard_map/while/body/eval_jaxpr/while/body/eval_jaxpr/hqk,qhd->khd/dot_general | solution.py:135
  504.9 7.8 bitcast_add_fusion.5
  514.0 3.6 broadcast_in_dim.59
  522.6 3.8 convolution_convert_fusion.5
  526.6 6.1 convolution_convert_fusion.4
  533.5 6.0 convolution_convert_fusion.3
  541.8 3.7 convolution_convert_fusion.2
  545.8 7.7 fusion.95
  553.4 5.6 fusion.94
  559.1 14.5 %fusion.93 = f32[1024,2048]{1,0:T(8,128)} fusion(bf16[1024,2048]{1,0:T(8,128)(2,1)} %all-gather.9.cloned.1.call-done, bf16[2048,2048]{1,0:T(8,128)(2,1)} %all-gather.19.cloned.1.call-done), kind=kOutput, calls=%fused_computation.160 | convolution fusion | flops 8589934592 | bytes 20971520 | tf_op jit(solution)/shard_map/dot_general | solution.py:215
  573.6 18.8 %convert_reduce_fusion = (f32[2048]{0:T(1024)S(1)}, bf16[1024,2048]{1,0:T(8,128)(2,1)S(1)}) fusion(f32[1024,2048]{1,0:T(8,128)} %fusion.93, f32[2048]{0:T(1024)S(1)} %convert_element_type.197, bf16[1024,2048]{1,0:T(8,128)(2,1)} %all-gather.23.cloned.1.call-done, bf16[2048,2048]{1,0:T(8,128)(2,1)} %all-gather.21.cloned.1.call-done), kind=kOutput, calls=%fused_computation.83 | convolution fusion | flops 8638167040 | bytes 25182208 | tf_op jit(solution)/shard_map/dot_general | solution.py:57
  592.4 1.9 copy-done.38
  594.3 13.8 %fusion.96 = f32[1024,2048]{1,0:T(8,128)} fusion(bf16[1024,2048]{1,0:T(8,128)(2,1)S(1)} %get-tuple-element.338, bf16[2048,2048]{1,0:T(8,128)(2,1)} %all-gather.19.cloned.1.call-done), kind=kOutput, calls=%fused_computation.163 | convolution fusion | flops 8589934592 | bytes 20971520 | tf_op jit(solution)/shard_map/dot_general | solution.py:57
  608.1 11.4 add_convert_fusion
  619.6 16.1 %fusion.91 = f32[1024,2048]{1,0:T(8,128)S(1)} fusion(bf16[2048,2048]{1,0:T(8,128)(2,1)} %all-gather.21.cloned.1.call-done, f32[1024,2048]{1,0:T(8,128)} %fusion.93, f32[2048]{0:T(1024)S(1)} %convert_element_type.197), kind=kOutput, calls=%fused_computation.159 | convolution fusion | flops 8610906112 | bytes 25174016 | tf_op jit(solution)/shard_map/dot_general | solution.py:228
  635.7 4.4 add_convert_fusion.1
  640.1 14.1 %convolution_convert_fusion.1 = bf16[2048,2048]{1,0:T(8,128)(2,1)} fusion(bf16[1024,2048]{1,0:T(8,128)(2,1)} %all-gather.9.cloned.1.call-done, bf16[1024,2048]{1,0:T(8,128)(2,1)} %copy-done.38), kind=kOutput, calls=%fused_computation.88 | convolution fusion | flops 8594128896 | bytes 16777216 | tf_op jit(solution)/shard_map/dot_general | solution.py:63
  654.3 16.1 %convolution_convert_fusion = bf16[2048,2048]{1,0:T(8,128)(2,1)} fusion(bf16[1024,2048]{1,0:T(8,128)(2,1)} %all-gather.23.cloned.1.call-done, f32[1024,2048]{1,0:T(8,128)} %fusion.93, f32[2048]{0:T(1024)S(1)} %convert_element_type.197), kind=kOutput, calls=%fused_computation.87 | convolution fusion | flops 8615100416 | bytes 20979712 | tf_op jit(solution)/shard_map/dot_general | solution.py:63
  671.4 1.9 convert_element_type.216
  673.2 3.7 reduce-scatter.15.cloned.1.call-done
  678.7 69.7 %reduce-scatter.17.cloned.1.call-done = bf16[256,512]{1,0:T(8,128)(2,1)} async-done(((bf16[2048,512]{1,0:T(8,128)(2,1)}), bf16[256,512]{1,0:T(8,128)(2,1)}) %reduce-scatter.17.cloned.1.call-update) | async-done | bytes 262160 | tf_op jit(solution)/shard_map/reduce_scatter | solution.py:278
  750.2 69.5 %reduce-scatter.19.cloned.1.call-done = bf16[512,256]{1,0:T(8,128)(2,1)} async-done(((bf16[512,2048]{1,0:T(8,128)(2,1)}), bf16[512,256]{1,0:T(8,128)(2,1)}) %reduce-scatter.19.cloned.1.call-update) | async-done | bytes 262160 | tf_op jit(solution)/shard_map/reduce_scatter | solution.py:292
  821.5 35.3 %all-reduce.1 = (f32[512]{0:T(512)}, f32[512]{0:T(512)}, f32[512]{0:T(512)}, f32[2048]{0:T(1024)}) all-reduce(f32[512]{0:T(512)S(1)} %reduce_sum.130, f32[512]{0:T(512)S(1)} %reduce_sum.132, f32[512]{0:T(512)S(1)} %reduce_sum.134, f32[2048]{0:T(1024)S(1)} %get-tuple-element.337), channel_id=1, replica_groups=mesh['dp'=8,'tensor'=4] {'dp'}, use_global_device_ids=true, to_apply=%region_19.20 | all-reduce | flops 3584 | bytes 28672 | tf_op jit(solution)/shard_map/psum | solution.py:305
  856.8 9.1 reduce-scatter.11.cloned.1.call-done
  865.9 2.3 fusion.86
  868.2 44.7 %reduce-scatter.9.cloned.1.call-done = bf16[256,2048]{1,0:T(8,128)(2,1)} async-done(((bf16[1024,2048]{1,0:T(8,128)(2,1)}), bf16[256,2048]{1,0:T(8,128)(2,1)}) %reduce-scatter.9.cloned.1.call-update) | async-done | bytes 1048592 | tf_op jit(solution)/shard_map/reduce_scatter | solution.py:231
  912.9 4.5 convert_reduce_fusion.3
  917.4 43.0 %all-reduce = (f32[2048]{0:T(1024)}, f32[2048]{0:T(1024)}, f32[2048]{0:T(1024)S(1)}) all-reduce(f32[2048]{0:T(1024)S(1)} %get-tuple-element.284, f32[2048]{0:T(1024)S(1)} %get-tuple-element.287, f32[2048]{0:T(1024)S(1)} %get-tuple-element.355), channel_id=1, replica_groups=mesh['dp'=8,'tensor'=4] {'dp','tensor'}, use_global_device_ids=true, to_apply=%region_14.15 | all-reduce | flops 6144 | bytes 49152 | tf_op jit(solution)/shard_map/psum | solution.py:321
  960.4 104.5 %reduce-scatter.21.cloned.1.call-done = bf16[256,2048]{1,0:T(8,128)(2,1)} async-done(((bf16[2048,2048]{1,0:T(8,128)(2,1)}), bf16[256,2048]{1,0:T(8,128)(2,1)}) %reduce-scatter.21.cloned.1.call-update) | async-done | bytes 1048592 | tf_op jit(solution)/shard_map/reduce_scatter | solution.py:284
  1064.9 2.8 convert_element_type.227
  1067.7 147.7 %reduce-scatter.23.cloned.1.call-done = bf16[2048,256]{1,0:T(8,128)(2,1)} async-done(((bf16[2048,2048]{1,0:T(8,128)(2,1)}), bf16[2048,256]{1,0:T(8,128)(2,1)}) %reduce-scatter.23.cloned.1.call-update) | async-done | bytes 1048592 | tf_op jit(solution)/shard_map/reduce_scatter | solution.py:298
  1215.4 2.7 convert_element_type.230
  (188 shorter events, 42.1 us)
Async XLA Ops:
  7.2 54.8 %all-gather.11.cloned.1.call-start = ((), (), s32[]{:S(2)}) async-start(), calls=%async_computation.9 | async-start | bytes 2359296 | tf_op jit(solution)/shard_map/all_gather | solution.py:196
  7.9 89.2 %all-gather.9.cloned.1.call-start = ((), (), s32[]{:S(2)}) async-start(), calls=%async_computation.8 | async-start | bytes 5242880 | tf_op jit(solution)/shard_map/all_gather | solution.py:194
  8.7 3.9 copy-start.18
  10.8 9.1 copy-start.31
  10.8 9.1 copy-start.32
  10.8 9.8 copy-start.33
  10.8 1.7 copy-start.20
  12.5 0.6 copy-start.25
  15.8 132.6 %all-gather.13.cloned.1.call-start = ((), (), s32[]{:S(2)}) async-start(), calls=%async_computation.10 | async-start | bytes 2359296 | tf_op jit(solution)/shard_map/all_gather | solution.py:197
  16.5 182.7 %all-gather.17.cloned.1.call-start = ((), (), s32[]{:S(2)}) async-start(), calls=%async_computation.12 | async-start | bytes 2359296 | tf_op jit(solution)/shard_map/all_gather | solution.py:202
  17.1 216.2 %all-gather.23.cloned.1.call-start = ((), (), s32[]{:S(2)}) async-start(), calls=%async_computation.16 | async-start | bytes 5242880 | tf_op jit(solution)/shard_map/all_gather | solution.py:236
  17.7 266.8 %all-gather.15.cloned.1.call-start = ((), (), s32[]{:S(2)}) async-start(), calls=%async_computation.11 | async-start | bytes 2359296 | tf_op jit(solution)/shard_map/all_gather | solution.py:198
  18.2 540.8 %all-gather.19.cloned.1.call-start = ((), (), s32[]{:S(2)}) async-start(), calls=%async_computation.13 | async-start | bytes 9437184 | tf_op jit(solution)/shard_map/all_gather | solution.py:199
  19.0 554.6 %all-gather.21.cloned.1.call-start = ((), (), s32[]{:S(2)}) async-start(), calls=%async_computation.14 | async-start | bytes 9437184 | tf_op jit(solution)/shard_map/all_gather | solution.py:203
  19.7 651.6 %reduce-scatter.13.cloned.1.call-start = ((), (), s32[]{:S(2)}) async-start(), calls=%async_computation.18 | async-start | bytes 2359296 | tf_op jit(solution)/shard_map/reduce_scatter | solution.py:266
  20.9 132.8 %copy-start.13 = (f32[1024,16]{0,1:T(8,128)}, f32[1024,16]{0,1:T(8,128)S(1)}, u32[]{:S(2)}) copy-start(f32[1024,16]{0,1:T(8,128)S(1)} %get-tuple-element.362) | copy-start | bytes 196612
  20.9 132.8 %copy-start.15 = (f32[1024,16]{0,1:T(8,128)}, f32[1024,16]{0,1:T(8,128)S(1)}, u32[]{:S(2)}) copy-start(f32[1024,16]{0,1:T(8,128)S(1)} %get-tuple-element.363) | copy-start | bytes 196612
  239.5 5.2 copy-start.9
  248.4 41.3 %copy-start.6 = (bf16[2,512,8,64]{1,3,2,0:T(8,128)(2,1)S(1)}, bf16[2,512,8,64]{1,3,2,0:T(8,128)(2,1)}, u32[]{:S(2)}) copy-start(bf16[2,512,8,64]{1,3,2,0:T(8,128)(2,1)} %custom-call.3) | copy-start | bytes 3145732
  248.4 41.3 %copy-start.17 = (f32[2,8,512]{2,1,0:T(8,128)S(1)}, f32[2,8,512]{2,1,0:T(8,128)}, u32[]{:S(2)}) copy-start(f32[2,8,512]{2,1,0:T(8,128)} %custom-call.4) | copy-start | bytes 98308
  321.2 1.0 copy-start.7
  385.3 23.5 %copy-start = (f32[1024,8,64]{0,2,1:T(8,128)S(1)}, f32[1024,8,64]{0,2,1:T(8,128)}, u32[]{:S(2)}) copy-start(f32[1024,8,64]{0,2,1:T(8,128)} %get-tuple-element.544) | copy-start | bytes 6291460 | tf_op jit(solution)/shard_map/while/body/eval_jaxpr/while
  416.6 1.3 copy-start.1
  480.6 24.3 %copy-start = (f32[1024,8,64]{0,2,1:T(8,128)S(1)}, f32[1024,8,64]{0,2,1:T(8,128)}, u32[]{:S(2)}) copy-start(f32[1024,8,64]{0,2,1:T(8,128)} %get-tuple-element.544) | copy-start | bytes 6291460 | tf_op jit(solution)/shard_map/while/body/eval_jaxpr/while
  512.7 1.3 copy-start.1
  514.0 5.1 copy-start.14
  514.0 5.1 copy-start.16
  517.6 5.0 copy-start.34
  521.7 1.0 copy-start.10
  521.7 4.9 copy-start.12
  526.5 150.4 %reduce-scatter.15.cloned.1.call-start = ((), (), s32[]{:S(2)}) async-start(), calls=%async_computation.19 | async-start | bytes 2359296 | tf_op jit(solution)/shard_map/reduce_scatter | solution.py:272
  526.5 6.1 copy-start.2
  532.6 215.8 %reduce-scatter.17.cloned.1.call-start = ((), (), s32[]{:S(2)}) async-start(), calls=%async_computation.20 | async-start | bytes 2359296 | tf_op jit(solution)/shard_map/reduce_scatter | solution.py:278
  533.5 6.1 copy-start.28
  533.5 6.1 copy-start.8
  539.5 280.2 %reduce-scatter.19.cloned.1.call-start = ((), (), s32[]{:S(2)}) async-start(), calls=%async_computation.21 | async-start | bytes 2359296 | tf_op jit(solution)/shard_map/reduce_scatter | solution.py:292
  539.6 2.2 copy-start.35
  545.5 320.4 %reduce-scatter.11.cloned.1.call-start = ((), (), s32[]{:S(2)}) async-start(), calls=%async_computation.17 | async-start | bytes 5242880 | tf_op jit(solution)/shard_map/reduce_scatter | solution.py:262
  545.7 7.7 copy-start.11
  545.7 7.7 copy-start.36
  592.4 1.9 copy-start.38
  594.3 13.8 %copy-start.4 = (f32[1024,2048]{1,0:T(8,128)S(1)}, f32[1024,2048]{1,0:T(8,128)}, u32[]{:S(2)}) copy-start(f32[1024,2048]{1,0:T(8,128)} %fusion.94) | copy-start | bytes 25165828
  619.5 293.4 %reduce-scatter.9.cloned.1.call-start = ((), (), s32[]{:S(2)}) async-start(), calls=%async_computation.15 | async-start | bytes 5242880 | tf_op jit(solution)/shard_map/reduce_scatter | solution.py:231
  619.6 16.1 %copy-start.37 = (bf16[512,2048]{1,0:T(8,128)(2,1)S(1)}, bf16[512,2048]{1,0:T(8,128)(2,1)}, u32[]{:S(2)}) copy-start(bf16[512,2048]{1,0:T(8,128)(2,1)} %all-gather.17.cloned.1.call-done) | copy-start | bytes 6291460
  640.1 424.8 %reduce-scatter.21.cloned.1.call-start = ((), (), s32[]{:S(2)}) async-start(), calls=%async_computation.22 | async-start | bytes 9437184 | tf_op jit(solution)/shard_map/reduce_scatter | solution.py:284
  654.3 561.1 %reduce-scatter.23.cloned.1.call-start = ((), (), s32[]{:S(2)}) async-start(), calls=%async_computation.23 | async-start | bytes 9437184 | tf_op jit(solution)/shard_map/reduce_scatter | solution.py:298
  670.4 0.7 copy-start.29
  670.4 0.7 copy-start.30
  670.4 0.7 copy-start.24
  670.4 0.8 copy-start.23
  670.4 0.9 copy-start.22
  670.4 195.4 %copy-start.3 = (bf16[256,2048]{1,0:T(8,128)(2,1)S(1)}, bf16[256,2048]{1,0:T(8,128)(2,1)}, u32[]{:S(2)}) copy-start(bf16[256,2048]{1,0:T(8,128)(2,1)} %param.21) | copy-start | bytes 3145732
  670.5 195.4 %copy-start.19 = (f32[2048]{0:T(1024)S(1)}, f32[2048]{0:T(1024)}, u32[]{:S(2)}) copy-start(f32[2048]{0:T(1024)} %copy-done.18) | copy-start | bytes 24580
  670.5 195.4 %copy-start.21 = (f32[256]{0:T(256)S(1)}, f32[256]{0:T(256)}, u32[]{:S(2)}) copy-start(f32[256]{0:T(256)} %copy-done.20) | copy-start | bytes 3076
  670.5 195.4 %copy-start.26 = (f32[256]{0:T(256)S(1)}, f32[256]{0:T(256)}, u32[]{:S(2)}) copy-start(f32[256]{0:T(256)} %copy-done.25) | copy-start | bytes 3076
  671.1 241.8 %copy-start.5 = (bf16[256,2048]{1,0:T(8,128)(2,1)S(1)}, bf16[256,2048]{1,0:T(8,128)(2,1)}, u32[]{:S(2)}) copy-start(bf16[256,2048]{1,0:T(8,128)(2,1)} %param.37) | copy-start | bytes 3145732
  960.4 258.3 %copy-start.27 = (f32[2048]{0:T(1024)}, f32[2048]{0:T(1024)S(1)}, u32[]{:S(2)}) copy-start(f32[2048]{0:T(1024)S(1)} %get-tuple-element.601) | copy-start | bytes 24580
Sparse Core Ops, SparseCore 0:
  10.1 51.8 all-gather.10
  64.1 32.9 all-gather.8
  99.2 49.0 all-gather.12
  150.3 48.8 all-gather.16
  200.6 32.6 all-gather.22
  235.2 49.1 all-gather.14
  286.5 122.9 all-gather.18
  411.6 123.1 all-gather.20
  538.9 66.6 reduce-scatter.12
  609.5 67.3 reduce-scatter.14
  681.0 67.3 reduce-scatter.16
  751.8 67.9 reduce-scatter.18
  822.3 43.5 reduce-scatter.10
  868.3 44.5 reduce-scatter.8
  916.3 148.5 reduce-scatter.20
  1068.4 146.9 reduce-scatter.22
where the time goes:
time: 1240 us; the launch traced here: 1230 us
  waiting for transfers between devices  687 us (55%)
  matrix products  330 us (27%)
  blocking collectives  78.3 us (6%)
  local copies, waits for them, and re-layouts  67.5 us (5%)
  other arithmetic  46.7 us (4%)
  between operations  15.4 us (1%)
    reduce_scatter x1, waiting for transfers between devices, on_device(): lax.psum_scatter(contract_first(activated, cot_all).astype(jnp.bfloat16),...  148 us
    reduce_scatter x1, waiting for transfers between devices, on_device(): lax.psum_scatter(contract_first(normed_all, grad_hidden).astype(jnp.bfloa...  104 us
    reduce_scatter x1, waiting for transfers between devices, on_device(): lax.psum_scatter(contract_first(normed_all, grad_v).astype(jnp.bfloat16),...  69.7 us
    reduce_scatter x1, waiting for transfers between devices, on_device(): lax.psum_scatter(contract_first(attended_flat, cot_all).astype(jnp.bfloat...  69.5 us
    dot_general x6, matrix products, contract_last(): lax.dot_general(left, right, (((1,), (1,)), ((), ())), preferred_element_...  63.5 us
    dot_general x6, matrix products, contract_first(): lax.dot_general(left, right, (((0,), (0,)), ((), ())), preferred_element_...  49.8 us
    dot_general x2, matrix products, one_block(): jnp.einsum('hqk,qhd->khd', grad_scores, query_rows, preferred_element_typ...  47.7 us
    all_gather x1, waiting for transfers between devices, on_device(): lax.all_gather(key_weight, 'dp', axis=0, tiled=True)  45.9 us
  transfers between devices with their start and end apart: 16, of which 13 were waited for; matrix products, arithmetic and copies ran while one was open for 35% of the time, Pallas kernels for 0%

commit v1 on v0

--- a/solution.py
+++ b/solution.py
@@ -191,7 +191,24 @@
     inv_scale = lax.rsqrt(jnp.mean(centred * centred, -1, keepdims=True) + EPS)
     standard = centred * inv_scale
     normed = (standard * gain_wide + norm_bias.astype(jnp.float32)).astype(jnp.bfloat16)
-    normed_all = lax.all_gather(normed, "tensor", axis=0, tiled=True)
+    size, index, width = (lax.axis_size("tensor"), lax.axis_index("tensor"), normed.shape[0])
+    upward = [(i, (i + 1) % size) for i in range(size)]
+    behind = [(i, (i - 1) % size) for i in range(size)]
+    result = jnp.zeros((*normed.shape[:0], size * width, *normed.shape[0 + 1 :]), normed.dtype)
+    result = lax.dynamic_update_slice_in_dim(result, normed, index * width, axis=0)
+    from_left = from_right = normed
+    middle = size // 2
+    for step in range(1, middle + 1):
+        from_left = lax.ppermute(from_left, "tensor", upward)
+        result = lax.dynamic_update_slice_in_dim(
+            result, from_left, (index - step) % size * width, axis=0
+        )
+        if step < size - middle:
+            from_right = lax.ppermute(from_right, "tensor", behind)
+            result = lax.dynamic_update_slice_in_dim(
+                result, from_right, (index + step) % size * width, axis=0
+            )
+    normed_all = result
     full_query, full_key, full_value, full_up = (
         lax.all_gather(query_weight, "dp", axis=0, tiled=True),
         lax.all_gather(key_weight, "dp", axis=0, tiled=True),

time: 1240 us -> 1200 us (0.968)
  waiting for transfers between devices: 687 us -> 646 us
    all_gather x1, waiting for transfers between devices: 45.9 us -> 5.67 us  [on_device(): lax.all_gather(key_weight, 'dp', axis=0, tiled=True)]
    all_gather x1 -> x0, waiting for transfers between devices: 35.1 us -> none  [on_device(): normed_all = lax.all_gather(normed, 'tensor', axis=0, tiled=True)]
    ppermute x0 -> x3, waiting for transfers between devices: none -> 29.4 us  [the longest x2 29.4 us: on_device(): from_left = lax.ppermute(from_left, 'tensor', upward)]
    all_gather x1, waiting for transfers between devices: 41.2 us -> 14.3 us  [on_device(): lax.all_gather(output_weight, 'dp', axis=1, tiled=True)]
    reduce_scatter x1, waiting for transfers between devices: 3.65 us -> 29 us  [on_device(): lax.psum_scatter(contract_first(normed_all, grad_k).astype(jnp.bfloat16),...]
  transfers between devices with their start and end apart: 16 -> 18, of which waited for: 13 -> 14; matrix products, arithmetic and copies ran while one was open for 35% -> 36% of each run, Pallas kernels for 0% -> 0%
where the time goes in v1:
time: 1200 us; the launch traced here: 1190 us
  waiting for transfers between devices  646 us (54%)
  matrix products  332 us (28%)
  blocking collectives  78.3 us (7%)
  local copies, waits for them, and re-layouts  69 us (6%)
  other arithmetic  41.5 us (3%)
  between operations  15.5 us (1%)
    reduce_scatter x1, waiting for transfers between devices, on_device(): lax.psum_scatter(contract_first(activated, cot_all).astype(jnp.bfloat16),...  148 us
    reduce_scatter x1, waiting for transfers between devices, on_device(): lax.psum_scatter(contract_first(normed_all, grad_hidden).astype(jnp.bfloa...  104 us
    reduce_scatter x1, waiting for transfers between devices, on_device(): lax.psum_scatter(contract_first(attended_flat, cot_all).astype(jnp.bfloat...  69.7 us
    reduce_scatter x1, waiting for transfers between devices, on_device(): lax.psum_scatter(contract_first(normed_all, grad_v).astype(jnp.bfloat16),...  69.5 us
    dot_general x6, matrix products, contract_last(): lax.dot_general(left, right, (((1,), (1,)), ((), ())), preferred_element_...  63.6 us
    dot_general x6, matrix products, contract_first(): lax.dot_general(left, right, (((0,), (0,)), ((), ())), preferred_element_...  50.1 us
    dot_general x2, matrix products, one_block(): jnp.einsum('hqk,qhd->khd', grad_scores, query_rows, preferred_element_typ...  48.7 us
    dot_general x2, matrix products, one_block(): jnp.einsum('hqk,khd->qhd', grad_scores, keys_rot, preferred_element_type=...  45 us
  transfers between devices with their start and end apart: 18, of which 14 were waited for; matrix products, arithmetic and copies ran while one was open for 36% of the time, Pallas kernels for 0%

profile of v1, /device:TPU:0, one launch (start us, length us, event | category | flops | bytes accessed | tf_op | source)
XLA Modules:
  0.0 1188.8 jit_solution(17435784464138922135)
XLA Ops:
  15.6 1.9 copy-done.7
  20.8 20.2 %collective-permute-done = bf16[256,2048]{1,0:T(8,128)(2,1)S(1)} collective-permute-done((bf16[256,2048]{1,0:T(8,128)(2,1)S(1)}, bf16[256,2048]{1,0:T(8,128)(2,1)S(1)}, u32[]{:S(2)}, u32[]{:S(2)}) %collective-permute-start) | collective-permute-done | bytes 1048608 | tf_op jit(solution)/shard_map/ppermute | solution.py:202
  41.0 2.5 collective-permute-start.2
  46.1 9.2 collective-permute-done.2
  56.3 5.7 all-gather.10.cloned.1.call-done
  62.0 5.2 convolution_add_fusion
  68.6 43.1 %all-gather.8.cloned.1.call-done = bf16[2048,512]{1,0:T(8,128)(2,1)} async-done(((bf16[256,512]{1,0:T(8,128)(2,1)}), bf16[2048,512]{1,0:T(8,128)(2,1)}) %all-gather.8.cloned.1.call-update) | async-done | bytes 2097168 | tf_op jit(solution)/shard_map/all_gather | solution.py:213
  111.7 5.4 convolution_add_fusion.1
  119.5 42.0 %all-gather.12.cloned.1.call-done = bf16[2048,512]{1,0:T(8,128)(2,1)} async-done(((bf16[256,512]{1,0:T(8,128)(2,1)}), bf16[2048,512]{1,0:T(8,128)(2,1)}) %all-gather.12.cloned.1.call-update) | async-done | bytes 2097168 | tf_op jit(solution)/shard_map/all_gather | solution.py:215
  161.5 5.2 add_convert_fusion.2
  166.8 31.3 %while.48 = (s32[]{:T(128)}, bf16[2,512,8,64]{1,3,2,0:T(8,128)(2,1)S(1)}, f32[2,8,512]{2,1,0:T(8,128)S(1)}, s32[2,512]{1,0:T(2,128)S(1)}, pred[2,512]{1,0:T(4,12...) while((s32[]{:T(128)}, ...), condition=%wide.region_5.6_spmd.clone, body=%wide.region_2.5_spmd.clone.sunk | while | flops 1125913600 | bytes 55723644 | solution.py:98
  168.2 4.7 fusion.156
  172.9 4.2 fusion.157
  177.2 5.4 fusion.158
  183.8 4.7 fusion.156
  188.4 4.2 fusion.157
  192.7 5.4 fusion.158
  198.1 14.3 %all-gather.14.cloned.1.call-done = bf16[512,2048]{1,0:T(8,128)(2,1)} async-done(((bf16[512,256]{1,0:T(8,128)(2,1)}), bf16[512,2048]{1,0:T(8,128)(2,1)}) %all-gather.14.cloned.1.call-update) | async-done | bytes 2097168 | tf_op jit(solution)/shard_map/all_gather | solution.py:219
  212.4 34.0 %all-gather.20.cloned.1.call-done = bf16[1024,2048]{1,0:T(8,128)(2,1)} async-done(((bf16[256,2048]{1,0:T(8,128)(2,1)}), bf16[1024,2048]{1,0:T(8,128)(2,1)}) %all-gather.20.cloned.1.call-update) | async-done | bytes 4194320 | tf_op jit(solution)/shard_map/all_gather | solution.py:253
  246.4 6.2 convolution_convert_fusion.6
  252.6 2.8 reshape.466
  255.4 2.2 copy.42
  257.7 193.8 %while.49 = (s32[]{:T(128)}, f32[1024,8,64]{0,2,1:T(8,128)}, f32[1024,8,64]{0,2,1:T(8,128)}, f32[2,512,8,64]{1,0,3,2:T(2,128)}, bf16[2,512,8,64]{1,3,2,0:T(8,128...) while((s32[]{:T(128)}, f32[1024,8,64]{0,2,1:T(8,128)}, ...), condition=%wide.region_9.10_spmd.clone, body=%wide.region_7.9_spmd.clone.sunk | while | flops 2746764288 | bytes 187764448 | solution.py:147
  259.1 9.5 subtract_exponential_fusion.3
  268.6 9.2 fusion.169
  277.8 22.0 %fusion.170 = f32[1,512,8,64]{1,3,2,0:T(8,128)S(1)} fusion(bf16[1024,8,64]{0,2,1:T(8,128)(2,1)} %get-tuple-element.565, f32[8,512,1024]{2,1,0:T(8,128)} %subtract_exponential_fusion.3, f32[8,512,1024]{2,1,0:T(8,128)} %fusion.169), kind=kOutput, calls=%fused_computation.45.clone.1 | convolution fusion | flops 557847552 | bytes 35651584 | tf_op jit(solution)/shard_map/while/body/eval_jaxpr/while/body/eval_jaxpr/hqk,khd->qhd/dot_general | solution.py:132
  300.9 19.6 %dynamic_update_slice.55 = f32[2,512,8,64]{1,0,3,2:T(2,128)} dynamic-update-slice(f32[2,512,8,64]{1,0,3,2:T(2,128)} %get-tuple-element.547, f32[1,512,8,64]{1,0,3,2:T(1,128)S(1)} %copy.64, s32[]{:T(128)} %get-tuple-element.544, s32[]{:T(128)} %constant.152.clone.1..sunk, s32[]{:T(128)} %constant.152.clone.1..sunk, s32[]{:T(128)} %constant.152.clone.1..sunk) | dynamic-update-slice | bytes 2097156 | tf_op jit(solution)/shard_map/while/body/eval_jaxpr/while/body/jit(dynamic_update_index_in_dim)/dynamic_update_slice | solution.py:147
  320.5 23.6 %bitcast_add_fusion.4 = f32[1024,8,64]{0,2,1:T(8,128)} fusion(f32[1024,8,64]{0,2,1:T(8,128)} %get-tuple-element.545, f32[8,512,1024]{2,1,0:T(8,128)} %subtract_exponential_fusion.3, f32[8,512,1024]{2,1,0:T(8,128)} %fusion.169, pred[]{:T(512)S(6)} %compare.10, bf16[2,512,8,64]{1,3,2,0:T(8,128)(2,1)} %get-tuple-element.562, s32[]{:T(128)} %get-tuple-element.544), kind=kOutput, calls=%fused_computation.43.clone.1 | convolution fusion | flops 558896128 | bytes 71827968 | tf_op jit(solution)/shard_map/while/body/eval_jaxpr/while/body/eval_jaxpr/hqk,qhd->khd/dot_general | solution.py:135
  344.1 8.1 bitcast_add_fusion.5
  354.8 9.5 subtract_exponential_fusion.3
  364.3 9.2 fusion.169
  373.5 23.0 %fusion.170 = f32[1,512,8,64]{1,3,2,0:T(8,128)S(1)} fusion(bf16[1024,8,64]{0,2,1:T(8,128)(2,1)} %get-tuple-element.565, f32[8,512,1024]{2,1,0:T(8,128)} %subtract_exponential_fusion.3, f32[8,512,1024]{2,1,0:T(8,128)} %fusion.169), kind=kOutput, calls=%fused_computation.45.clone.1 | convolution fusion | flops 557847552 | bytes 35651584 | tf_op jit(solution)/shard_map/while/body/eval_jaxpr/while/body/eval_jaxpr/hqk,khd->qhd/dot_general | solution.py:132
  397.5 19.6 %dynamic_update_slice.55 = f32[2,512,8,64]{1,0,3,2:T(2,128)} dynamic-update-slice(f32[2,512,8,64]{1,0,3,2:T(2,128)} %get-tuple-element.547, f32[1,512,8,64]{1,0,3,2:T(1,128)S(1)} %copy.64, s32[]{:T(128)} %get-tuple-element.544, s32[]{:T(128)} %constant.152.clone.1..sunk, s32[]{:T(128)} %constant.152.clone.1..sunk, s32[]{:T(128)} %constant.152.clone.1..sunk) | dynamic-update-slice | bytes 2097156 | tf_op jit(solution)/shard_map/while/body/eval_jaxpr/while/body/jit(dynamic_update_index_in_dim)/dynamic_update_slice | solution.py:147
  417.1 25.1 %bitcast_add_fusion.4 = f32[1024,8,64]{0,2,1:T(8,128)} fusion(f32[1024,8,64]{0,2,1:T(8,128)} %get-tuple-element.545, f32[8,512,1024]{2,1,0:T(8,128)} %subtract_exponential_fusion.3, f32[8,512,1024]{2,1,0:T(8,128)} %fusion.169, pred[]{:T(512)S(6)} %compare.10, bf16[2,512,8,64]{1,3,2,0:T(8,128)(2,1)} %get-tuple-element.562, s32[]{:T(128)} %get-tuple-element.544), kind=kOutput, calls=%fused_computation.43.clone.1 | convolution fusion | flops 558896128 | bytes 71827968 | tf_op jit(solution)/shard_map/while/body/eval_jaxpr/while/body/eval_jaxpr/hqk,qhd->khd/dot_general | solution.py:135
  442.2 7.9 bitcast_add_fusion.5
  451.4 3.6 broadcast_in_dim.62
  460.1 3.8 convolution_convert_fusion.5
  464.0 6.1 convolution_convert_fusion.4
  471.0 6.0 convolution_convert_fusion.3
  479.3 3.7 convolution_convert_fusion.2
  483.3 7.7 fusion.96
  491.0 5.6 fusion.95
  496.6 14.5 %fusion.94 = f32[1024,2048]{1,0:T(8,128)} fusion(bf16[1024,2048]{1,0:T(8,128)(2,1)} %constant_dynamic-update-slice_fusion, bf16[2048,2048]{1,0:T(8,128)(2,1)} %all-gather.16.cloned.1.call-done), kind=kOutput, calls=%fused_computation.164 | convolution fusion | flops 8589934592 | bytes 20971520 | tf_op jit(solution)/shard_map/dot_general | solution.py:232
  511.1 18.7 %convert_reduce_fusion = (f32[2048]{0:T(1024)S(1)}, bf16[1024,2048]{1,0:T(8,128)(2,1)S(1)}) fusion(f32[1024,2048]{1,0:T(8,128)} %fusion.94, f32[2048]{0:T(1024)S(1)} %convert_element_type.197, bf16[1024,2048]{1,0:T(8,128)(2,1)} %all-gather.20.cloned.1.call-done, bf16[2048,2048]{1,0:T(8,128)(2,1)} %all-gather.18.cloned.1.call-done), kind=kOutput, calls=%fused_computation.83 | convolution fusion | flops 8638167040 | bytes 25182208 | tf_op jit(solution)/shard_map/dot_general | solution.py:57
  529.8 2.0 copy-done.42
  531.8 14.0 %fusion.97 = f32[1024,2048]{1,0:T(8,128)} fusion(bf16[1024,2048]{1,0:T(8,128)(2,1)S(1)} %get-tuple-element.338, bf16[2048,2048]{1,0:T(8,128)(2,1)} %all-gather.16.cloned.1.call-done), kind=kOutput, calls=%fused_computation.167 | convolution fusion | flops 8589934592 | bytes 20971520 | tf_op jit(solution)/shard_map/dot_general | solution.py:57
  545.8 11.4 add_convert_fusion
  557.3 16.1 %fusion.91 = f32[1024,2048]{1,0:T(8,128)S(1)} fusion(bf16[2048,2048]{1,0:T(8,128)(2,1)} %all-gather.18.cloned.1.call-done, f32[1024,2048]{1,0:T(8,128)} %fusion.94, f32[2048]{0:T(1024)S(1)} %convert_element_type.197), kind=kOutput, calls=%fused_computation.163 | convolution fusion | flops 8610906112 | bytes 25174016 | tf_op jit(solution)/shard_map/dot_general | solution.py:245
  573.5 4.3 add_convert_fusion.1
  577.9 14.2 %convolution_convert_fusion.1 = bf16[2048,2048]{1,0:T(8,128)(2,1)} fusion(bf16[1024,2048]{1,0:T(8,128)(2,1)} %constant_dynamic-update-slice_fusion, bf16[1024,2048]{1,0:T(8,128)(2,1)} %copy-done.42), kind=kOutput, calls=%fused_computation.88 | convolution fusion | flops 8594128896 | bytes 16777216 | tf_op jit(solution)/shard_map/dot_general | solution.py:63
  592.2 16.3 %convolution_convert_fusion = bf16[2048,2048]{1,0:T(8,128)(2,1)} fusion(bf16[1024,2048]{1,0:T(8,128)(2,1)} %all-gather.20.cloned.1.call-done, f32[1024,2048]{1,0:T(8,128)} %fusion.94, f32[2048]{0:T(1024)S(1)} %convert_element_type.197), kind=kOutput, calls=%fused_computation.87 | convolution fusion | flops 8615100416 | bytes 20979712 | tf_op jit(solution)/shard_map/dot_general | solution.py:63
  611.3 29.0 %reduce-scatter.15.cloned.1.call-done = bf16[256,512]{1,0:T(8,128)(2,1)} async-done(((bf16[2048,512]{1,0:T(8,128)(2,1)}), bf16[256,512]{1,0:T(8,128)(2,1)}) %reduce-scatter.15.cloned.1.call-update) | async-done | bytes 262160 | tf_op jit(solution)/shard_map/reduce_scatter | solution.py:289
  642.1 69.5 %reduce-scatter.17.cloned.1.call-done = bf16[256,512]{1,0:T(8,128)(2,1)} async-done(((bf16[2048,512]{1,0:T(8,128)(2,1)}), bf16[256,512]{1,0:T(8,128)(2,1)}) %reduce-scatter.17.cloned.1.call-update) | async-done | bytes 262160 | tf_op jit(solution)/shard_map/reduce_scatter | solution.py:295
  713.4 69.7 %reduce-scatter.19.cloned.1.call-done = bf16[512,256]{1,0:T(8,128)(2,1)} async-done(((bf16[512,2048]{1,0:T(8,128)(2,1)}), bf16[512,256]{1,0:T(8,128)(2,1)}) %reduce-scatter.19.cloned.1.call-update) | async-done | bytes 262160 | tf_op jit(solution)/shard_map/reduce_scatter | solution.py:309
  784.9 35.3 %all-reduce.1 = (f32[512]{0:T(512)}, f32[512]{0:T(512)}, f32[512]{0:T(512)}, f32[2048]{0:T(1024)}) all-reduce(f32[512]{0:T(512)S(1)} %reduce_sum.130, f32[512]{0:T(512)S(1)} %reduce_sum.132, f32[512]{0:T(512)S(1)} %reduce_sum.134, f32[2048]{0:T(1024)S(1)} %get-tuple-element.337), channel_id=1, replica_groups=mesh['dp'=8,'tensor'=4] {'dp'}, use_global_device_ids=true, to_apply=%region_19.20 | all-reduce | flops 3584 | bytes 28672 | tf_op jit(solution)/shard_map/psum | solution.py:322
  820.2 8.9 reduce-scatter.11.cloned.1.call-done
  829.1 2.3 fusion.86
  831.4 44.8 %reduce-scatter.9.cloned.1.call-done = bf16[256,2048]{1,0:T(8,128)(2,1)} async-done(((bf16[1024,2048]{1,0:T(8,128)(2,1)}), bf16[256,2048]{1,0:T(8,128)(2,1)}) %reduce-scatter.9.cloned.1.call-update) | async-done | bytes 1048592 | tf_op jit(solution)/shard_map/reduce_scatter | solution.py:248
  876.2 4.5 convert_reduce_fusion.3
  880.8 43.0 %all-reduce = (f32[2048]{0:T(1024)}, f32[2048]{0:T(1024)}, f32[2048]{0:T(1024)S(1)}) all-reduce(f32[2048]{0:T(1024)S(1)} %get-tuple-element.284, f32[2048]{0:T(1024)S(1)} %get-tuple-element.287, f32[2048]{0:T(1024)S(1)} %get-tuple-element.357), channel_id=1, replica_groups=mesh['dp'=8,'tensor'=4] {'dp','tensor'}, use_global_device_ids=true, to_apply=%region_14.15 | all-reduce | flops 6144 | bytes 49152 | tf_op jit(solution)/shard_map/psum | solution.py:338
  923.8 104.5 %reduce-scatter.21.cloned.1.call-done = bf16[256,2048]{1,0:T(8,128)(2,1)} async-done(((bf16[2048,2048]{1,0:T(8,128)(2,1)}), bf16[256,2048]{1,0:T(8,128)(2,1)}) %reduce-scatter.21.cloned.1.call-update) | async-done | bytes 1048592 | tf_op jit(solution)/shard_map/reduce_scatter | solution.py:301
  1028.3 2.8 convert_element_type.227
  1031.1 147.7 %reduce-scatter.23.cloned.1.call-done = bf16[2048,256]{1,0:T(8,128)(2,1)} async-done(((bf16[2048,2048]{1,0:T(8,128)(2,1)}), bf16[2048,256]{1,0:T(8,128)(2,1)}) %reduce-scatter.23.cloned.1.call-update) | async-done | bytes 1048592 | tf_op jit(solution)/shard_map/reduce_scatter | solution.py:315
  1178.8 2.7 convert_element_type.230
  (203 shorter events, 44.9 us)
Async XLA Ops:
  7.2 6.9 copy-start.3
  7.2 54.8 %all-gather.10.cloned.1.call-start = ((), (), s32[]{:S(2)}) async-start(), calls=%async_computation.9 | async-start | bytes 2359296 | tf_op jit(solution)/shard_map/all_gather | solution.py:214
  7.9 103.8 %all-gather.8.cloned.1.call-start = ((), (), s32[]{:S(2)}) async-start(), calls=%async_computation.8 | async-start | bytes 2359296 | tf_op jit(solution)/shard_map/all_gather | solution.py:213
  8.7 152.9 %all-gather.12.cloned.1.call-start = ((), (), s32[]{:S(2)}) async-start(), calls=%async_computation.10 | async-start | bytes 2359296 | tf_op jit(solution)/shard_map/all_gather | solution.py:215
  9.4 203.0 %all-gather.14.cloned.1.call-start = ((), (), s32[]{:S(2)}) async-start(), calls=%async_computation.11 | async-start | bytes 2359296 | tf_op jit(solution)/shard_map/all_gather | solution.py:219
  10.0 236.4 %all-gather.20.cloned.1.call-start = ((), (), s32[]{:S(2)}) async-start(), calls=%async_computation.15 | async-start | bytes 5242880 | tf_op jit(solution)/shard_map/all_gather | solution.py:253
  10.6 486.0 %all-gather.16.cloned.1.call-start = ((), (), s32[]{:S(2)}) async-start(), calls=%async_computation.12 | async-start | bytes 9437184 | tf_op jit(solution)/shard_map/all_gather | solution.py:216
  11.1 500.0 %all-gather.18.cloned.1.call-start = ((), (), s32[]{:S(2)}) async-start(), calls=%async_computation.13 | async-start | bytes 9437184 | tf_op jit(solution)/shard_map/all_gather | solution.py:220
  11.9 3.7 copy-start.23
  14.0 1.5 copy-start.25
  14.5 3.0 copy-start.30
  14.5 5.6 copy-start.36
  14.5 5.6 copy-start.37
  14.5 6.3 copy-start.38
  15.6 1.9 copy-start.7
  17.5 23.5 %collective-permute-start = (bf16[256,2048]{1,0:T(8,128)(2,1)S(1)}, bf16[256,2048]{1,0:T(8,128)(2,1)S(1)}, u32[]{:S(2)}, u32[]{:S(2)}) collective-permute-start(bf16[256,2048]{1,0:T(8,128)(2,1)S(1)} %get-tuple-element.346), channel_id=1, source_target_pairs={{0,1},{1,2},{2,3},{3,0},{4,5},{5,6},{6,7},{7,4},{8,9},{9,10},{10,1... | collective-permute-start | bytes 3145736 | tf_op jit(solution)/shard_map/ppermute | solution.py:202
  18.0 27.0 %collective-permute-start.1 = (bf16[256,2048]{1,0:T(8,128)(2,1)S(1)}, bf16[256,2048]{1,0:T(8,128)(2,1)S(1)}, u32[]{:S(2)}, u32[]{:S(2)}) collective-permute-start(bf16[256,2048]{1,0:T(8,128)(2,1)S(1)} %get-tuple-element.346), channel_id=1, source_target_pairs={{0,3},{1,0},{2,1},{3,2},{4,7},{5,4},{6,5},{7,6},{8,11},{9,8},{10,9... | collective-permute-start | bytes 3145736 | tf_op jit(solution)/shard_map/ppermute | solution.py:207
  20.0 589.5 %reduce-scatter.13.cloned.1.call-start = ((), (), s32[]{:S(2)}) async-start(), calls=%async_computation.17 | async-start | bytes 2359296 | tf_op jit(solution)/shard_map/reduce_scatter | solution.py:283
  41.0 14.2 %collective-permute-start.2 = (bf16[256,2048]{1,0:T(8,128)(2,1)S(1)}, bf16[256,2048]{1,0:T(8,128)(2,1)S(1)}, u32[]{:S(2)}, u32[]{:S(2)}) collective-permute-start(bf16[256,2048]{1,0:T(8,128)(2,1)S(1)} %collective-permute-done), channel_id=1, source_target_pairs={{0,1},{1,2},{2,3},{3,0},{4,5},{5,6},{6,7},{7,4},{8,9},{9,10},{10,1... | collective-permute-start | bytes 3145736 | tf_op jit(solution)/shard_map/ppermute | solution.py:202
  43.9 73.3 %copy-start.18 = (f32[1024,16]{0,1:T(8,128)}, f32[1024,16]{0,1:T(8,128)S(1)}, u32[]{:S(2)}) copy-start(f32[1024,16]{0,1:T(8,128)S(1)} %get-tuple-element.364) | copy-start | bytes 196612
  43.9 73.3 %copy-start.20 = (f32[1024,16]{0,1:T(8,128)}, f32[1024,16]{0,1:T(8,128)S(1)}, u32[]{:S(2)}) copy-start(f32[1024,16]{0,1:T(8,128)S(1)} %get-tuple-element.365) | copy-start | bytes 196612
  67.2 1.3 copy-start.10
  111.7 5.5 copy-start.11
  119.5 47.2 %copy-start.12 = (bf16[2,512,8,64]{1,3,2,0:T(8,128)(2,1)S(1)}, bf16[2,512,8,64]{1,3,2,0:T(8,128)(2,1)}, u32[]{:S(2)}) copy-start(bf16[2,512,8,64]{1,3,2,0:T(8,128)(2,1)} %custom-call.3) | copy-start | bytes 3145732
  119.5 47.2 %copy-start.22 = (f32[2,8,512]{2,1,0:T(8,128)S(1)}, f32[2,8,512]{2,1,0:T(8,128)}, u32[]{:S(2)}) copy-start(f32[2,8,512]{2,1,0:T(8,128)} %custom-call.4) | copy-start | bytes 98308
  198.1 48.3 %copy-start.6 = (bf16[2,512,8,64]{1,3,2,0:T(8,128)(2,1)}, bf16[2,512,8,64]{1,3,2,0:T(8,128)(2,1)S(1)}, u32[]{:S(2)}) copy-start(bf16[2,512,8,64]{1,3,2,0:T(8,128)(2,1)S(1)} %get-tuple-element.626) | copy-start | bytes 3145732
  198.1 48.3 %copy-start.13 = (bf16[2,512,8,64]{1,3,2,0:T(8,128)(2,1)}, bf16[2,512,8,64]{1,3,2,0:T(8,128)(2,1)S(1)}, u32[]{:S(2)}) copy-start(bf16[2,512,8,64]{1,3,2,0:T(8,128)(2,1)S(1)} %get-tuple-element.189) | copy-start | bytes 3145732
  320.5 23.6 %copy-start = (f32[1024,8,64]{0,2,1:T(8,128)S(1)}, f32[1024,8,64]{0,2,1:T(8,128)}, u32[]{:S(2)}) copy-start(f32[1024,8,64]{0,2,1:T(8,128)} %get-tuple-element.546) | copy-start | bytes 6291460 | tf_op jit(solution)/shard_map/while/body/eval_jaxpr/while
  352.3 1.3 copy-start.1
  417.1 25.1 %copy-start = (f32[1024,8,64]{0,2,1:T(8,128)S(1)}, f32[1024,8,64]{0,2,1:T(8,128)}, u32[]{:S(2)}) copy-start(f32[1024,8,64]{0,2,1:T(8,128)} %get-tuple-element.546) | copy-start | bytes 6291460 | tf_op jit(solution)/shard_map/while/body/eval_jaxpr/while
  450.1 1.3 copy-start.1
  451.4 5.1 copy-start.19
  451.4 5.1 copy-start.21
  455.1 5.0 copy-start.8
  459.2 1.0 copy-start.15
  459.2 4.9 copy-start.17
  464.0 176.3 %reduce-scatter.15.cloned.1.call-start = ((), (), s32[]{:S(2)}) async-start(), calls=%async_computation.18 | async-start | bytes 2359296 | tf_op jit(solution)/shard_map/reduce_scatter | solution.py:289
  464.0 6.1 copy-start.2
  470.1 241.5 %reduce-scatter.17.cloned.1.call-start = ((), (), s32[]{:S(2)}) async-start(), calls=%async_computation.19 | async-start | bytes 2359296 | tf_op jit(solution)/shard_map/reduce_scatter | solution.py:295
  471.0 6.1 copy-start.33
  471.0 6.1 copy-start.14
  477.0 306.1 %reduce-scatter.19.cloned.1.call-start = ((), (), s32[]{:S(2)}) async-start(), calls=%async_computation.20 | async-start | bytes 2359296 | tf_op jit(solution)/shard_map/reduce_scatter | solution.py:309
  477.1 2.3 copy-start.39
  483.0 346.1 %reduce-scatter.11.cloned.1.call-start = ((), (), s32[]{:S(2)}) async-start(), calls=%async_computation.16 | async-start | bytes 5242880 | tf_op jit(solution)/shard_map/reduce_scatter | solution.py:279
  483.3 7.7 copy-start.16
  483.3 7.7 copy-start.41
  529.8 2.0 copy-start.42
  531.8 14.0 %copy-start.5 = (f32[1024,2048]{1,0:T(8,128)S(1)}, f32[1024,2048]{1,0:T(8,128)}, u32[]{:S(2)}) copy-start(f32[1024,2048]{1,0:T(8,128)} %fusion.95) | copy-start | bytes 25165828
  557.3 319.0 %reduce-scatter.9.cloned.1.call-start = ((), (), s32[]{:S(2)}) async-start(), calls=%async_computation.14 | async-start | bytes 5242880 | tf_op jit(solution)/shard_map/reduce_scatter | solution.py:248
  557.3 16.1 %copy-start.40 = (bf16[512,2048]{1,0:T(8,128)(2,1)S(1)}, bf16[512,2048]{1,0:T(8,128)(2,1)}, u32[]{:S(2)}) copy-start(bf16[512,2048]{1,0:T(8,128)(2,1)} %all-gather.14.cloned.1.call-done) | copy-start | bytes 6291460
  577.8 450.4 %reduce-scatter.21.cloned.1.call-start = ((), (), s32[]{:S(2)}) async-start(), calls=%async_computation.21 | async-start | bytes 9437184 | tf_op jit(solution)/shard_map/reduce_scatter | solution.py:301
  592.2 586.6 %reduce-scatter.23.cloned.1.call-start = ((), (), s32[]{:S(2)}) async-start(), calls=%async_computation.22 | async-start | bytes 9437184 | tf_op jit(solution)/shard_map/reduce_scatter | solution.py:315
  608.5 0.7 copy-start.34
  608.5 0.7 copy-start.35
  608.5 0.7 copy-start.29
  608.5 0.8 copy-start.28
  608.5 0.9 copy-start.27
  608.5 220.6 %copy-start.4 = (bf16[256,2048]{1,0:T(8,128)(2,1)S(1)}, bf16[256,2048]{1,0:T(8,128)(2,1)}, u32[]{:S(2)}) copy-start(bf16[256,2048]{1,0:T(8,128)(2,1)} %param.21) | copy-start | bytes 3145732
  608.5 220.6 %copy-start.24 = (f32[2048]{0:T(1024)S(1)}, f32[2048]{0:T(1024)}, u32[]{:S(2)}) copy-start(f32[2048]{0:T(1024)} %copy-done.23) | copy-start | bytes 24580
  608.5 220.6 %copy-start.26 = (f32[256]{0:T(256)S(1)}, f32[256]{0:T(256)}, u32[]{:S(2)}) copy-start(f32[256]{0:T(256)} %copy-done.25) | copy-start | bytes 3076
  608.5 220.6 %copy-start.31 = (f32[256]{0:T(256)S(1)}, f32[256]{0:T(256)}, u32[]{:S(2)}) copy-start(f32[256]{0:T(256)} %copy-done.30) | copy-start | bytes 3076
  609.2 267.1 %copy-start.9 = (bf16[256,2048]{1,0:T(8,128)(2,1)S(1)}, bf16[256,2048]{1,0:T(8,128)(2,1)}, u32[]{:S(2)}) copy-start(bf16[256,2048]{1,0:T(8,128)(2,1)} %param.37) | copy-start | bytes 3145732
  923.8 258.3 %copy-start.32 = (f32[2048]{0:T(1024)}, f32[2048]{0:T(1024)S(1)}, u32[]{:S(2)}) copy-start(f32[2048]{0:T(1024)S(1)} %get-tuple-element.603) | copy-start | bytes 24580
Sparse Core Ops, SparseCore 0:
  10.1 51.7 all-gather.9
  64.1 47.6 all-gather.7
  113.9 47.6 all-gather.11
  163.4 48.9 all-gather.13
  213.8 32.5 all-gather.19
  248.4 124.4 all-gather.15
  374.9 123.1 all-gather.17
  502.2 66.5 reduce-scatter.12
  572.9 67.3 reduce-scatter.14
  644.2 67.3 reduce-scatter.16
  715.1 67.9 reduce-scatter.18
  785.5 43.5 reduce-scatter.10
  831.6 44.5 reduce-scatter.8
  879.7 148.5 reduce-scatter.20
  1031.8 146.9 reduce-scatter.22
